TPU v7x, 512 devices: a whole 4x8x8 slice. The times are simulated.
512 devices in a mesh: grp: 128 (over y, x_lo, z), blk: 4 (over x_hi, core).
Axes of the slice: x: 4 (x_hi: 2, x_lo: 2; x = x_hi * 2 + x_lo), y: 8, z: 8, core: 2. Of those that a mesh axis runs over, the one named last changes fastest.
Arguments:
- amplitudes: bfloat16 [2048, 128, 512], P('grp', 'blk'), may hold values from -6 to 6
- integrals: float32 [2048, 12, 128, 128], P(('grp', 'blk')), may hold values from -0.15625 to 0.15625
- tile_rows: int32 [2048, 12], P(('grp', 'blk')), may hold values from 0 to 2047, as said below
- destinations: int32 [2048, 4], replicated, may hold values from 0 to 127, as said below
- source_terms: bfloat16 [262144, 512], P(('grp', 'blk')), may hold values from -6 to 6
- occ_energy: float32 [512], replicated, may hold values from 0.5 to 4
- virt_energy: float32 [262144], P(('grp', 'blk')), may hold values from 0.5 to 4
Outputs:
- new_amplitudes: bfloat16 [262144, 512], P(('grp', 'blk'))
Inputs may be any that keep to these rules, and one draw needn't show every extreme that they name: `destinations`: each row names 4 different groups. Every group is named by exactly 64 rows in all. Among the 16 rows k of one owning group k // 16, no group is named by more than 2 rows, and that many is reached. `tile_rows`: the 12 entries of a row are different.
All inputs are finite; a program needn't handle non-finite values.
Results may differ from a plain program's by a relative error of at most 0.001.
Values may be sent and summed in bfloat16 or wider, within the bound.
No kernel may reach another device: no remote copies, remote signals or barrier semaphores. Data moves between devices by JAX's collectives and lax.ppermute only.
A program may use at most 64 MiB of HBM per device.

v0:
```python
import jax
import jax.numpy as jnp
from jax import lax
from jax.sharding import PartitionSpec as P

DEST = 4


def per_device(
    amplitudes, integrals, tile_rows, destinations, source_terms, occ_energy, virt_energy
):
    groups = lax.axis_size("grp")
    own_group = lax.axis_index("grp")
    owned_tiles = amplitudes.shape[0]
    quarter = amplitudes.shape[1]
    pair_width = amplitudes.shape[2]
    all_tiles = destinations.shape[0]
    slot_count = max(2, owned_tiles * DEST // groups)
    my_dest = lax.dynamic_slice_in_dim(destinations, own_group * owned_tiles, owned_tiles, 0)
    targets = jnp.arange(groups, dtype=jnp.int32)
    named_mine = jnp.any(my_dest[:, :, None] == targets[None, None, :], axis=1).astype(jnp.int32)
    before = jnp.cumsum(named_mine, axis=0) - named_mine
    slot_of = jnp.take_along_axis(before, my_dest, axis=1)
    send_place = my_dest * slot_count + slot_of
    select = jnp.any(
        jnp.arange(groups * slot_count, dtype=jnp.int32)[:, None, None] == send_place[None, :, :],
        axis=2,
    )
    select = select.astype(jnp.bfloat16)
    outgoing = jnp.dot(
        select,
        amplitudes.reshape(owned_tiles, quarter * pair_width),
        preferred_element_type=jnp.float32,
    )
    outgoing = outgoing.astype(jnp.bfloat16).reshape(groups * slot_count, quarter, pair_width)
    named_all = jnp.any(destinations == own_group, axis=1).astype(jnp.int32)
    per_source = named_all.reshape(groups, owned_tiles)
    slot_all = (jnp.cumsum(per_source, axis=1) - per_source).reshape(all_tiles)
    source_of = jnp.arange(all_tiles, dtype=jnp.int32) // owned_tiles
    position = source_of * slot_count + slot_all
    compact_of = jnp.cumsum(named_all) - named_all
    received = owned_tiles * DEST
    matches = (compact_of[None, :] == jnp.arange(received, dtype=jnp.int32)[:, None]) & (
        named_all[None, :] == 1
    )
    pick_rows = jnp.sum(jnp.where(matches, position[None, :], 0), axis=1)
    delivered = named_all[tile_rows]
    slots_used = jnp.where(delivered == 1, compact_of[tile_rows], 0)
    weights = integrals * delivered.astype(jnp.float32)[:, :, None, None]
    columns, row_tiles = tile_rows.shape
    tile_size = integrals.shape[3]
    flat_slots = slots_used.reshape(columns * row_tiles)
    incoming = lax.all_to_all(outgoing, "grp", split_axis=0, concat_axis=0, tiled=True)
    gathered_rows = jnp.take(incoming, pick_rows, axis=0)
    arrived = lax.all_gather(gathered_rows, "blk", axis=1, tiled=True)
    rows_here = arrived.shape[1]
    width_here = arrived.shape[2]
    picked = jnp.take(arrived, flat_slots, axis=0).reshape(
        columns, row_tiles, rows_here, width_here
    )
    picked = picked.astype(jnp.float32)
    ladder = jnp.einsum("crqk,crqp->ckp", weights, picked, precision=lax.Precision.HIGHEST)
    ladder = ladder.reshape(columns * tile_size, pair_width)
    denominator = virt_energy[:, None] + occ_energy[None, :]
    return ((source_terms.astype(jnp.float32) + ladder) / denominator).astype(jnp.bfloat16)


def solution(mesh):
    in_specs = (
        P("grp", "blk", None),
        P(("grp", "blk"), None, None, None),
        P(("grp", "blk"), None),
        P(),
        P(("grp", "blk"), None),
        P(),
        P(("grp", "blk")),
    )
    out_specs = P(("grp", "blk"), None)
    return jax.shard_map(
        per_device, mesh=mesh, in_specs=in_specs, out_specs=out_specs, check_vma=False
    )
```

profile of v0, /device:TPU:1, one launch (start us, length us, event | category | flops | bytes accessed | tf_op | source)
XLA Modules:
  0.0 397.3 jit_solution(89998441502436940)
XLA Ops:
  6.5 0.8 constant_dynamic-slice_fusion
  7.7 0.1 copy.23
  7.8 0.1 reshape.189
  7.8 0.8 gather_fusion.4
  8.8 0.1 fusion.9
  8.9 0.3 copy.29
  9.2 5.6 %convolution_convert_fusion = bf16[256,16384]{1,0:T(8,128)(2,1)} fusion(pred[256,16]{0,1:T(8,128)(4,1)S(1)} %fusion.9, bf16[16,16384]{1,0:T(8,128)(2,1)S(1)} %bitcast.35), kind=kOutput, calls=%fused_computation.5 | convolution fusion | flops 138412032 | bytes 8916992 | tf_op jit(solution)/shard_map/dot_general | solution.py:30
  14.8 10.4 %copy.30 = bf16[32,8,32,512]{3,2,1,0:T(8,128)(2,1)} copy(bf16[32,8,32,512]{3,1,2,0:T(8,128)(2,1)} %bitcast.33) | data formatting | bytes 16777216
  25.2 19.9 %all-to-all-start = ((bf16[256,32,512]{2,1,0:T(8,128)(2,1)}), bf16[256,32,512]{2,1,0:T(8,128)(2,1)}, u32[]{:S(2)}, u32[]{:S(2)}) async-start(bf16[256,32,512]{2,1,0:T(8,128)(2,1)} %bitcast.32), calls=%async_computation | async-start | bytes 16777216 | tf_op jit(solution)/shard_map/all_to_all | solution.py:53
  45.2 0.2 all-gather.2.cloned.1.call-start
  45.6 0.1 copy.19
  45.8 0.1 reduce_window_sum.46
  45.8 0.3 reduce-window.9
  46.2 0.1 slice_reduce_fusion
  46.4 0.2 select_reduce_fusion
  46.7 220.9 %all-to-all-done = bf16[256,32,512]{2,1,0:T(8,128)(2,1)} async-done(((bf16[256,32,512]{2,1,0:T(8,128)(2,1)}), bf16[256,32,512]{2,1,0:T(8,128)(2,1)}, u32[]{:S(2)}, u32[]{:S(2)}) %all-to-all-start) | async-done | bytes 8388640 | tf_op jit(solution)/shard_map/all_to_all | solution.py:53
  267.6 4.1 %gather_fusion.2 = bf16[64,32,512]{2,1,0:T(8,128)(2,1)S(1)} fusion(bf16[256,32,512]{2,1,0:T(8,128)(2,1)} %all-to-all-done, s32[1024]{0:T(1024)S(1)} %pad_clamp_fusion.1), kind=kCustom, calls=%fused_computation.2 | custom fusion | bytes 4194560 | tf_op jit(solution)/shard_map/jit(_take)/gather | solution.py:54
  271.6 1.6 broadcast_select_fusion
  273.4 0.8 gather_fusion.1
  274.2 0.8 gather_fusion
  275.2 100.1 %all-gather.2.cloned.1.call-done = bf16[64,128,512]{2,1,0:T(8,128)(2,1)} async-done(((bf16[64,32,512]{2,1,0:T(8,128)(2,1)}), bf16[64,128,512]{2,1,0:T(8,128)(2,1)}) %all-gather.2.cloned.1.call-update) | async-done | bytes 8388624 | tf_op jit(solution)/shard_map/all_gather | solution.py:55
  375.3 8.4 %gather_fusion.3 = bf16[48,128,512]{2,1,0:T(8,128)(2,1)} fusion(bf16[64,128,512]{2,1,0:T(8,128)(2,1)} %all-gather.2.cloned.1.call-done, s32[1024]{0:T(1024)S(1)} %pad_clamp_fusion), kind=kCustom, calls=%fused_computation.3 | custom fusion | bytes 12583104 | tf_op jit(solution)/shard_map/jit(_take)/gather | solution.py:58
  383.7 5.7 %fusion = f32[4,128,512,1]{2,1,3,0:T(8,128)S(1)} fusion(bf16[4,12,128,512]{3,2,1,0:T(8,128)(2,1)} %bitcast.34, pred[4,12]{1,0:T(4,128)(4,1)S(1)} %compare_and_fusion.1, f32[4,12,128,128]{3,2,1,0:T(8,128)S(1)} %copy-done.6, f32[4,12]{1,0:T(4,128)S(1)} %reshape.199), kind=kOutput, calls=%fused_computation.6 | convolution fusion | flops 4835770368 | bytes 10486000 | tf_op jit(solution)/shard_map/crqk,crqp->ckp/dot_general | solution.py:62
  389.4 1.0 fusion.7
  (46 shorter events, 1.2 us)
Async XLA Ops:
  6.5 2.4 copy-start
  25.2 20.2 %copy-start.2 = (s32[2048,4]{0,1:T(4,128)S(1)}, s32[2048,4]{0,1:T(4,128)}, u32[]{:S(2)}) copy-start(s32[2048,4]{0,1:T(4,128)} %param.10) | copy-start | bytes 98308
  25.2 242.4 %all-to-all-start = ((bf16[256,32,512]{2,1,0:T(8,128)(2,1)}), bf16[256,32,512]{2,1,0:T(8,128)(2,1)}, u32[]{:S(2)}, u32[]{:S(2)}) async-start(bf16[256,32,512]{2,1,0:T(8,128)(2,1)} %bitcast.32), calls=%async_computation | async-start | bytes 16777216 | tf_op jit(solution)/shard_map/all_to_all | solution.py:53
  45.2 228.2 %copy-start.3 = (s32[4,12]{1,0:T(4,128)S(1)}, s32[4,12]{1,0:T(4,128)}, u32[]{:S(2)}) copy-start(s32[4,12]{1,0:T(4,128)} %param.9) | copy-start | bytes 580
  45.2 330.1 %all-gather.2.cloned.1.call-start = ((), (), s32[]{:S(2)}) async-start(), calls=%async_computation.1 | async-start | bytes 10485760 | tf_op jit(solution)/shard_map/all_gather | solution.py:55
  275.2 108.5 %copy-start.6 = (f32[4,12,128,128]{3,2,1,0:T(8,128)S(1)}, f32[4,12,128,128]{3,2,1,0:T(8,128)}, u32[]{:S(2)}) copy-start(f32[4,12,128,128]{3,2,1,0:T(8,128)} %param.8) | copy-start | bytes 9437188
  383.7 5.7 %copy-start.1 = (bf16[512,512]{1,0:T(8,128)(2,1)S(1)}, bf16[512,512]{1,0:T(8,128)(2,1)}, u32[]{:S(2)}) copy-start(bf16[512,512]{1,0:T(8,128)(2,1)} %param.11) | copy-start | bytes 1572868
  383.7 5.7 %copy-start.4 = (f32[512]{0:T(512)S(1)}, f32[512]{0:T(512)}, u32[]{:S(2)}) copy-start(f32[512]{0:T(512)} %param.12) | copy-start | bytes 6148
  383.7 5.7 %copy-start.5 = (f32[512]{0:T(512)S(1)}, f32[512]{0:T(512)}, u32[]{:S(2)}) copy-start(f32[512]{0:T(512)} %param.13) | copy-start | bytes 6148
Sparse Core Ops, SparseCore 0:
  273.4 101.8 all-gather.1
where the time goes:
time: 398 us; the launch traced here: 397 us
  waiting for transfers between devices  321 us (81%)
  local copies, waits for them, and re-layouts  27.6 us (7%)
  starting transfers between devices  20.2 us (5%)
  between operations  13.6 us (3%)
  matrix products  11.3 us (3%)
    all_to_all x1, waiting for transfers between devices, per_device(): lax.all_to_all(outgoing, 'grp', split_axis=0, concat_axis=0, tiled=True)  221 us
    all_gather x1, waiting for transfers between devices, per_device(): arrived = lax.all_gather(gathered_rows, 'blk', axis=1, tiled=True)  100 us
    all_to_all x1, starting transfers between devices, per_device(): lax.all_to_all(outgoing, 'grp', split_axis=0, concat_axis=0, tiled=True)  19.9 us
    unnamed x17, local copies, waits for them, and re-layouts  10.8 us
    gather x1, local copies, waits for them, and re-layouts, per_device(): jnp.take(arrived, flat_slots, axis=0)  8.38 us
  transfers between devices with their start and end apart: 2, of which 2 were waited for; matrix products, arithmetic and copies ran while one was open for 1% of the time, Pallas kernels for 0%

commit v1 on v0

--- a/solution.py
+++ b/solution.py
@@ -52,7 +52,9 @@
     flat_slots = slots_used.reshape(columns * row_tiles)
     incoming = lax.all_to_all(outgoing, "grp", split_axis=0, concat_axis=0, tiled=True)
     gathered_rows = jnp.take(incoming, pick_rows, axis=0)
-    arrived = lax.all_gather(gathered_rows, "blk", axis=1, tiled=True)
+    arrived = jnp.concatenate(
+        lax.all_to_all(jnp.stack([gathered_rows] * lax.axis_size("blk")), "blk", 0, 0), axis=1
+    )
     rows_here = arrived.shape[1]
     width_here = arrived.shape[2]
     picked = jnp.take(arrived, flat_slots, axis=0).reshape(

time: 398 us -> 431 us (1.083)
  the two profiles are of different devices: /device:TPU:1 before, /device:TPU:32 now
where the time goes in v1:
time: 431 us; the launch traced here: 430 us
  waiting for transfers between devices  352 us (82%)
  local copies, waits for them, and re-layouts  40.2 us (9%)
  starting transfers between devices  24.8 us (6%)
  matrix products  11.3 us (3%)
    all_to_all x1, waiting for transfers between devices, per_device(): lax.all_to_all(outgoing, 'grp', split_axis=0, concat_axis=0, tiled=True)  259 us
    all_to_all x1, waiting for transfers between devices, per_device(): lax.all_to_all(jnp.stack([gathered_rows] * lax.axis_size('blk')), 'blk',...  92.6 us
    all_to_all x1, starting transfers between devices, per_device(): lax.all_to_all(outgoing, 'grp', split_axis=0, concat_axis=0, tiled=True)  18.9 us
    unnamed x17, local copies, waits for them, and re-layouts  10.8 us
  transfers between devices with their start and end apart: 2, of which 2 were waited for; matrix products, arithmetic and copies ran while one was open for 1% of the time, Pallas kernels for 0%

profile of v1, /device:TPU:32, one launch (start us, length us, event | category | flops | bytes accessed | tf_op | source)
XLA Modules:
  0.0 430.4 jit_solution(966563027569777628)
XLA Ops:
  0.0 0.8 constant_dynamic-slice_fusion
  1.2 0.1 reshape.199
  1.3 0.8 gather_fusion.4
  2.3 0.1 fusion.9
  2.4 0.3 copy.37
  2.7 5.6 %convolution_convert_fusion = bf16[256,16384]{1,0:T(8,128)(2,1)} fusion(pred[256,16]{0,1:T(8,128)(4,1)S(1)} %fusion.9, bf16[16,16384]{1,0:T(8,128)(2,1)S(1)} %bitcast.39), kind=kOutput, calls=%fused_computation.5 | convolution fusion | flops 138412032 | bytes 8916992 | tf_op jit(solution)/shard_map/dot_general | solution.py:30
  8.3 10.4 %copy.38 = bf16[32,8,32,512]{3,2,1,0:T(8,128)(2,1)} copy(bf16[32,8,32,512]{3,1,2,0:T(8,128)(2,1)} %bitcast.36) | data formatting | bytes 16777216
  18.7 18.9 %all-to-all-start = ((bf16[256,32,512]{2,1,0:T(8,128)(2,1)}), bf16[256,32,512]{2,1,0:T(8,128)(2,1)}, u32[]{:S(2)}, u32[]{:S(2)}) async-start(bf16[256,32,512]{2,1,0:T(8,128)(2,1)} %bitcast.35), calls=%async_computation | async-start | bytes 16777216 | tf_op jit(solution)/shard_map/all_to_all | solution.py:53
  37.6 0.3 reduce-window.9
  38.2 0.1 copy.26
  38.4 0.1 slice_reduce_fusion
  38.6 0.2 select_reduce_fusion
  38.8 259.0 %all-to-all-done = bf16[256,32,512]{2,1,0:T(8,128)(2,1)} async-done(((bf16[256,32,512]{2,1,0:T(8,128)(2,1)}), bf16[256,32,512]{2,1,0:T(8,128)(2,1)}, u32[]{:S(2)}, u32[]{:S(2)}) %all-to-all-start) | async-done | bytes 8388640 | tf_op jit(solution)/shard_map/all_to_all | solution.py:53
  297.8 4.1 gather_fusion.2
  301.9 0.3 broadcast_select_fusion
  302.2 4.3 stack.2
  306.4 6.0 %all-to-all-start.1 = ((bf16[4,64,32,512]{3,2,1,0:T(8,128)(2,1)}), bf16[4,64,32,512]{3,2,1,0:T(8,128)(2,1)}, u32[]{:S(2)}, u32[]{:S(2)}) async-start(bf16[4,64,32,512]{3,2,1,0:T(8,128)(2,1)} %stack.2), calls=%async_computation.1 | async-start | bytes 16777216 | tf_op jit(solution)/shard_map/all_to_all | solution.py:56
  312.5 0.8 gather_fusion
  313.3 0.8 gather_fusion.1
  314.3 92.6 %all-to-all-done.1 = bf16[4,64,32,512]{3,2,1,0:T(8,128)(2,1)} async-done(((bf16[4,64,32,512]{3,2,1,0:T(8,128)(2,1)}), bf16[4,64,32,512]{3,2,1,0:T(8,128)(2,1)}, u32[]{:S(2)}, u32[]{:S(2)}) %all-to-all-start.1) | async-done | bytes 8388640 | tf_op jit(solution)/shard_map/all_to_all | solution.py:56
  406.9 8.3 %copy.32 = bf16[4,64,32,512]{3,2,0,1:T(8,128)(2,1)} copy(bf16[4,64,32,512]{3,2,1,0:T(8,128)(2,1)} %all-to-all-done.1) | data formatting | bytes 16777216 | tf_op jit(solution)/shard_map/all_to_all | solution.py:56
  415.1 8.5 %gather_fusion.3 = bf16[48,128,512]{2,1,0:T(8,128)(2,1)} fusion(bf16[64,128,512]{2,1,0:T(8,128)(2,1)} %bitcast.37, s32[1024]{0:T(1024)S(1)} %pad_clamp_fusion), kind=kCustom, calls=%fused_computation.3 | custom fusion | bytes 12583104 | tf_op jit(solution)/shard_map/jit(_take)/gather | solution.py:60
  423.6 5.7 %fusion = f32[4,128,512,1]{2,1,3,0:T(8,128)S(1)} fusion(bf16[4,12,128,512]{3,2,1,0:T(8,128)(2,1)} %bitcast.38, pred[4,12]{1,0:T(4,128)(4,1)S(1)} %compare_and_fusion.1, f32[4,12,128,128]{3,2,1,0:T(8,128)S(1)} %copy-done.6, f32[4,12]{1,0:T(4,128)S(1)} %reshape.209), kind=kOutput, calls=%fused_computation.6 | convolution fusion | flops 4835770368 | bytes 10486000 | tf_op jit(solution)/shard_map/crqk,crqp->ckp/dot_general | solution.py:64
  429.4 1.0 fusion.7
  (47 shorter events, 1.4 us)
Async XLA Ops:
  0.0 2.4 copy-start
  18.7 18.9 %copy-start.2 = (s32[2048,4]{0,1:T(4,128)S(1)}, s32[2048,4]{0,1:T(4,128)}, u32[]{:S(2)}) copy-start(s32[2048,4]{0,1:T(4,128)} %param.10) | copy-start | bytes 98308
  18.7 279.1 %all-to-all-start = ((bf16[256,32,512]{2,1,0:T(8,128)(2,1)}), bf16[256,32,512]{2,1,0:T(8,128)(2,1)}, u32[]{:S(2)}, u32[]{:S(2)}) async-start(bf16[256,32,512]{2,1,0:T(8,128)(2,1)} %bitcast.35), calls=%async_computation | async-start | bytes 16777216 | tf_op jit(solution)/shard_map/all_to_all | solution.py:53
  306.4 6.0 %copy-start.3 = (s32[4,12]{1,0:T(4,128)S(1)}, s32[4,12]{1,0:T(4,128)}, u32[]{:S(2)}) copy-start(s32[4,12]{1,0:T(4,128)} %param.9) | copy-start | bytes 580
  306.4 100.4 %all-to-all-start.1 = ((bf16[4,64,32,512]{3,2,1,0:T(8,128)(2,1)}), bf16[4,64,32,512]{3,2,1,0:T(8,128)(2,1)}, u32[]{:S(2)}, u32[]{:S(2)}) async-start(bf16[4,64,32,512]{3,2,1,0:T(8,128)(2,1)} %stack.2), calls=%async_computation.1 | async-start | bytes 16777216 | tf_op jit(solution)/shard_map/all_to_all | solution.py:56
  415.1 8.5 %copy-start.6 = (f32[4,12,128,128]{3,2,1,0:T(8,128)S(1)}, f32[4,12,128,128]{3,2,1,0:T(8,128)}, u32[]{:S(2)}) copy-start(f32[4,12,128,128]{3,2,1,0:T(8,128)} %param.8) | copy-start | bytes 9437188
  423.6 5.7 %copy-start.1 = (bf16[512,512]{1,0:T(8,128)(2,1)S(1)}, bf16[512,512]{1,0:T(8,128)(2,1)}, u32[]{:S(2)}) copy-start(bf16[512,512]{1,0:T(8,128)(2,1)} %param.11) | copy-start | bytes 1572868
  423.6 5.7 %copy-start.4 = (f32[512]{0:T(512)S(1)}, f32[512]{0:T(512)}, u32[]{:S(2)}) copy-start(f32[512]{0:T(512)} %param.12) | copy-start | bytes 6148
  423.6 5.7 %copy-start.5 = (f32[512]{0:T(512)S(1)}, f32[512]{0:T(512)}, u32[]{:S(2)}) copy-start(f32[512]{0:T(512)} %param.13) | copy-start | bytes 6148
